TPU v7x, 32 devices: a whole 2x2x4 slice. The times are simulated.
32 devices in a mesh: trow: 4 (over y, x), tcol: 4 (over z), dp: 2 (over core).
Axes of the slice: x: 2, y: 2, z: 4, core: 2. Of those that a mesh axis runs over, the one named last changes fastest.
Arguments:
- embeds: bfloat16 [2048, 1024], P('dp'), may hold values from -6 to 6
- frequencies: bfloat16 [1024, 8192], P(None, ('trow', 'tcol')), may hold values from -0.5 to 0.5
- phases: float32 [8192], P(('trow', 'tcol')), may hold values from -3.140625 to 3.140625
- labels: int32 [2048], P('dp'), may hold values from 0 to 999
- weights: float32 [8192, 1000], P(('tcol', 'dp'), 'trow'), may hold values from -6 to 6
Outputs:
- gram_matrix: float32 [8192, 8192], P(('trow', 'dp'), 'tcol')
- new_weights: float32 [8192, 1000], P(('tcol', 'dp'), 'trow')
All inputs are finite; a program needn't handle non-finite values.
Results may differ from a plain program's by a relative error of at most 0.023.
Values may be sent and summed in bfloat16 or wider, within the bound.
No kernel may reach another device: no remote copies, remote signals or barrier semaphores. Data moves between devices by JAX's collectives and lax.ppermute only.
A program may use at most 128 MiB of HBM per device.

v0:
```python
import jax
import jax.numpy as jnp
from jax import lax
from jax.sharding import PartitionSpec as P

C = 1000
ROOT_TWO = 1.4142135623730951
RIDGE = 0.5
STEP_RATE = 0.5


def broadcast(array, axis, root):
    mine = lax.axis_index(axis) == root
    return lax.psum(jnp.where(mine, array, jnp.zeros_like(array)), axis)


def featurize(embeds, frequencies, phases):
    angles = jnp.dot(embeds, frequencies, preferred_element_type=jnp.float32) + phases
    return (ROOT_TWO * jnp.cos(angles)).astype(jnp.bfloat16)


def shards(embeds, frequencies, phases, labels, weights):
    rows_here = embeds.shape[0]
    n_row = lax.axis_size("trow")
    n_dp = lax.axis_size("dp")
    row_idx = lax.axis_index("trow")
    col_idx = lax.axis_index("tcol")
    dp_idx = lax.axis_index("dp")
    total_rows = rows_here * n_dp
    contract = (((0,), (0,)), ((), ()))
    own_part = featurize(embeds, frequencies, phases)
    left_feats = lax.all_gather(own_part, "tcol", axis=1, tiled=True)
    right_feats = broadcast(left_feats, "trow", col_idx)
    tile_width = left_feats.shape[1]
    sub_rows = tile_width // n_dp
    gram_part = lax.psum_scatter(
        (
            lax.dot_general(left_feats, right_feats, contract, preferred_element_type=jnp.float32)
            / total_rows
        ).astype(jnp.bfloat16),
        "dp",
        scatter_dimension=0,
        tiled=True,
    ).astype(jnp.float32)
    global_rows = row_idx * tile_width + dp_idx * sub_rows + jnp.arange(sub_rows, dtype=jnp.int32)
    global_cols = col_idx * tile_width + jnp.arange(tile_width, dtype=jnp.int32)
    gram_rows = gram_part + RIDGE * (global_rows[:, None] == global_cols[None, :]).astype(
        jnp.float32
    )
    class_width = weights.shape[1]
    class_ids = row_idx * class_width + jnp.arange(class_width, dtype=jnp.int32)
    onehot = (labels[:, None] == class_ids[None, :]).astype(jnp.bfloat16)
    label_term = lax.dot_general(
        right_feats, onehot, contract, preferred_element_type=jnp.float32
    ) * (C / total_rows)
    label_rows = lax.psum_scatter(
        label_term.astype(jnp.bfloat16), "dp", scatter_dimension=0, tiled=True
    ).astype(jnp.float32)
    gram_three = gram_rows.astype(jnp.bfloat16).reshape(sub_rows, n_dp, sub_rows)
    block_ids = jnp.arange(n_row, dtype=jnp.int32)
    local_weights = weights.astype(jnp.bfloat16)[None]
    pieces = lax.all_gather(local_weights, ("trow", "dp"), axis=0, tiled=True)
    positions = jnp.arange(pieces.shape[0], dtype=jnp.int32)
    sub_index = positions % n_dp
    owner_index = positions // n_dp
    chosen = jnp.take(gram_three, sub_index, axis=1)
    products = jnp.einsum("rpk,pkc->rpc", chosen, pieces, preferred_element_type=jnp.float32)
    placing = (owner_index[:, None] == block_ids[None, :]).astype(jnp.float32)
    folded = jnp.einsum("rpc,pi->ric", products, placing)
    curv_local = folded.reshape(sub_rows, n_row * class_width)
    diag_block = lax.dynamic_slice_in_dim(gram_rows, dp_idx * sub_rows, sub_rows, 1)
    diag_local = jnp.diagonal(diag_block) * (row_idx == col_idx).astype(jnp.float32)
    row_total = lax.psum(curv_local.astype(jnp.bfloat16), "tcol").astype(jnp.float32)
    received, diag_vals = (
        broadcast(row_total.astype(jnp.bfloat16), "trow", col_idx).astype(row_total.dtype),
        broadcast(diag_local.astype(jnp.bfloat16), "trow", col_idx).astype(diag_local.dtype),
    )
    curv_mine = lax.dynamic_slice_in_dim(received, row_idx * class_width, class_width, 1)
    updated = weights - STEP_RATE * (curv_mine - label_rows) / diag_vals[:, None]
    return (gram_rows, updated)


def solution(mesh):
    return jax.shard_map(
        shards,
        mesh=mesh,
        in_specs=(
            P("dp", None),
            P(None, ("trow", "tcol")),
            P(("trow", "tcol")),
            P("dp"),
            P(("tcol", "dp"), "trow"),
        ),
        out_specs=(P(("trow", "dp"), "tcol"), P(("tcol", "dp"), "trow")),
        check_vma=False,
    )
```

profile of v0, /device:TPU:0, one launch (start us, length us, event | category | flops | bytes accessed | tf_op | source)
XLA Modules:
  0.0 468.6 jit_solution(4243780087989902327)
XLA Ops:
  8.1 1.5 copy-done
  9.6 9.6 %multiply_convert_fusion.1 = bf16[1024,512]{1,0:T(8,128)(2,1)} fusion(bf16[1024,1024]{1,0:T(8,128)(2,1)S(1)} %copy-done, bf16[1024,512]{1,0:T(8,128)(2,1)} %param.6, f32[512]{0:T(512)} %param.7), kind=kOutput, calls=%fused_computation.19 | convolution fusion | flops 1075314688 | bytes 4196352 | tf_op jit(solution)/shard_map/dot_general | solution.py:18
  19.3 83.6 %all-gather.4.cloned.1.call-done = bf16[1024,2048]{1,0:T(8,128)(2,1)} async-done(((bf16[1024,512]{1,0:T(8,128)(2,1)}), bf16[1024,2048]{1,0:T(8,128)(2,1)}) %all-gather.4.cloned.1.call-update) | async-done | bytes 4194320 | tf_op jit(solution)/shard_map/all_gather | solution.py:32
  102.8 4.5 broadcast_select_fusion
  107.4 102.1 %all-reduce.4.cloned.1.call-done = bf16[1024,2048]{1,0:T(8,128)(2,1)} async-done(((bf16[1024,2048]{1,0:T(8,128)(2,1)}), bf16[1024,2048]{1,0:T(8,128)(2,1)}) %all-reduce.4.cloned.1.call-update) | async-done | bytes 4194320 | tf_op jit(solution)/shard_map/psum | solution.py:14
  209.5 14.0 %multiply_convert_fusion = bf16[2048,2048]{1,0:T(8,128)(2,1)} fusion(bf16[1024,2048]{1,0:T(8,128)(2,1)} %all-gather.4.cloned.1.call-done, bf16[1024,2048]{1,0:T(8,128)(2,1)} %all-reduce.4.cloned.1.call-done), kind=kOutput, calls=%fused_computation.7 | convolution fusion | flops 8598323200 | bytes 16777216 | tf_op jit(solution)/shard_map/dot_general | solution.py:38
  223.5 0.0 all-gather.6.cloned.1.call-start
  223.5 1.1 copy-done.2
  224.7 0.8 convert_element_type.51
  225.6 0.2 all-reduce.6.cloned.1.call-start
  225.9 14.2 %reduce-scatter.3.cloned.1.call-done = bf16[1024,2048]{1,0:T(8,128)(2,1)} async-done(((bf16[2048,2048]{1,0:T(8,128)(2,1)}), bf16[1024,2048]{1,0:T(8,128)(2,1)}) %reduce-scatter.3.cloned.1.call-update) | async-done | bytes 4194320 | tf_op jit(solution)/shard_map/reduce_scatter | solution.py:36
  240.0 5.8 %fusion.21 = (bf16[1024,2048]{1,0:T(8,128)(2,1)S(1)}, f32[1024,2048]{1,0:T(8,128)}) fusion(s32[2048]{0:T(1024)S(1)} %iota_add_fusion, s32[1024]{0:T(1024)S(1)} %iota_add_fusion.1, bf16[1024,2048]{1,0:T(8,128)(2,1)} %reduce-scatter.3.cloned.1.call-done), kind=kLoop, calls=%fused_computation.49 | loop fusion | flops 10485760 | bytes 16789504 | tf_op jit(solution)/shard_map/convert_element_type | solution.py:59
  245.8 0.6 fusion.22
  246.4 0.2 copy.24
  246.6 1.6 copy.25
  248.1 4.4 gather_fusion.2
  252.5 6.1 %gather_fusion.1 = bf16[8,512,1024]{2,1,0:T(8,128)(2,1)} fusion(bf16[512,2,1024]{2,0,1:T(8,128)(2,1)} %bitcast.32, s32[1024]{0:T(1024)S(1)} %pad_clamp_fusion), kind=kCustom, calls=%fused_computation.1 | custom fusion | bytes 16777248 | tf_op jit(solution)/shard_map/jit(_take)/gather | solution.py:66
  258.6 4.3 all-gather.6.cloned.1.call-done
  262.9 10.8 %fusion = bf16[8,1024,250]{1,2,0:T(8,128)(2,1)} fusion(bf16[8,1024,250]{2,1,0:T(8,128)(2,1)} %bitcast.37, bf16[512,8,1024]{2,0,1:T(8,128)(2,1)} %bitcast.33, bf16[512,8,1024]{2,0,1:T(8,128)(2,1)} %bitcast.34, pred[8]{0:T(512)(128)(4,1)S(1)} %compare_and_fusion), kind=kOutput, calls=%fused_computation.4 | convolution fusion | flops 4236247040 | bytes 24969224 | tf_op jit(solution)/shard_map/rpk,pkc->rpc/dot_general | solution.py:67
  273.8 6.2 %convert_bitcast_fusion = bf16[1024,4,250]{0,1,2:T(4,128)(2,1)} fusion(bf16[8,1024,250]{1,2,0:T(8,128)(2,1)} %fusion, s32[8]{0:T(128)S(1)} %and_select_fusion.2), kind=kOutput, calls=%fused_computation.21 | convolution fusion | flops 16384032 | bytes 6144032 | tf_op jit(solution)/shard_map/rpc,pi->ric/dot_general | solution.py:69
  280.0 5.1 %copy.12 = bf16[1024,4,250]{2,1,0:T(4,128)(2,1)S(1)} copy(bf16[1024,4,250]{0,1,2:T(4,128)(2,1)} %convert_bitcast_fusion) | data formatting | bytes 4096000 | tf_op jit(solution)/shard_map/convert_element_type | solution.py:73
  285.1 3.0 reshape.100
  288.1 0.0 reduce-scatter.5.cloned.1.call-start
  288.1 4.7 fusion.8
  292.8 0.0 all-reduce.8.cloned.1.call-start
  292.9 81.5 %all-reduce.6.cloned.1.call-done = bf16[1024,1000]{1,0:T(8,128)(2,1)} async-done(((bf16[1024,1000]{1,0:T(8,128)(2,1)}), bf16[1024,1000]{1,0:T(8,128)(2,1)}) %all-reduce.6.cloned.1.call-update) | async-done | bytes 2048016 | tf_op jit(solution)/shard_map/psum | solution.py:73
  374.3 3.1 broadcast_select_fusion.1
  377.5 4.9 %constant_dynamic-slice_fusion = f32[1024,1024]{1,0:T(8,128)} fusion(f32[1024,2048]{1,0:T(8,128)} %get-tuple-element.3, s32[]{:T(128)S(6)} %select_n.92), kind=kLoop, calls=%fused_computation.46 | loop fusion | bytes 8388612 | tf_op jit(solution)/shard_map/dynamic_slice | solution.py:71
  382.4 16.8 %gather_fusion = f32[1024]{0:T(1024)S(1)} fusion(f32[1024,1024]{1,0:T(8,128)} %constant_dynamic-slice_fusion, s32[1024]{0:T(1024)S(1)} %bitcast.30), kind=kCustom, calls=%fused_computation | custom fusion | bytes 16384 | tf_op jit(solution)/shard_map/jit(diagonal)/cond/branch_0_fun/gather | solution.py:72
  399.2 8.8 %psum.31 = bf16[1024]{0:T(1024)(128)(2,1)S(1)} all-reduce(bf16[1024]{0:T(1024)(128)(2,1)S(1)} %fusion.14), channel_id=1, replica_groups=mesh['trow'=4,'tcol'=4,'dp'=2] {'trow'}, use_global_device_ids=true, to_apply=%region_5.6 | all-reduce | flops 1024 | bytes 4096 | tf_op jit(solution)/shard_map/psum | solution.py:14
  408.0 50.5 %all-reduce.8.cloned.1.call-done = bf16[1024,1000]{1,0:T(8,128)(2,1)} async-done(((bf16[1024,1000]{1,0:T(8,128)(2,1)}), bf16[1024,1000]{1,0:T(8,128)(2,1)}) %all-reduce.8.cloned.1.call-update) | async-done | bytes 2048016 | tf_op jit(solution)/shard_map/psum | solution.py:14
  458.4 2.7 divide_subtract_fusion
  (27 shorter events, 0.3 us)
Async XLA Ops:
  8.0 1.6 copy-start
  8.0 94.8 %all-gather.4.cloned.1.call-start = ((), (), s32[]{:S(2)}) async-start(), calls=%async_computation.2 | async-start | bytes 5242880 | tf_op jit(solution)/shard_map/all_gather | solution.py:32
  19.2 190.3 %all-reduce.4.cloned.1.call-start = ((), (), s32[]{:S(2)}) async-start(), calls=%async_computation.3 | async-start | bytes 8388608 | tf_op jit(solution)/shard_map/psum | solution.py:14
  107.3 132.7 %reduce-scatter.3.cloned.1.call-start = ((), (), s32[]{:S(2)}) async-start(), calls=%async_computation.4 | async-start | bytes 12582912 | tf_op jit(solution)/shard_map/reduce_scatter | solution.py:36
  223.5 1.2 copy-start.2
  223.5 39.4 %all-gather.6.cloned.1.call-start = ((), (), s32[]{:S(2)}) async-start(), calls=%async_computation.8 | async-start | bytes 4718592 | tf_op jit(solution)/shard_map/all_gather | solution.py:62
  225.6 148.8 %all-reduce.6.cloned.1.call-start = ((), (), s32[]{:S(2)}) async-start(), calls=%async_computation.5 | async-start | bytes 4194304 | tf_op jit(solution)/shard_map/psum | solution.py:73
  280.0 8.2 %copy-start.3 = (s32[1024]{0:T(1024)S(1)}, s32[1024]{0:T(1024)}, u32[]{:S(2)}) copy-start(s32[1024]{0:T(1024)} %param.8) | copy-start | bytes 12292
  288.1 119.9 %reduce-scatter.5.cloned.1.call-start = ((), (), s32[]{:S(2)}) async-start(), calls=%async_computation.7 | async-start | bytes 1572864 | tf_op jit(solution)/shard_map/reduce_scatter | solution.py:56
  292.8 165.6 %all-reduce.8.cloned.1.call-start = ((), (), s32[]{:S(2)}) async-start(), calls=%async_computation.6 | async-start | bytes 4194304 | tf_op jit(solution)/shard_map/psum | solution.py:14
  377.5 83.7 %copy-start.1 = (bf16[1024,1024]{1,0:T(8,128)(2,1)S(1)}, bf16[1024,1024]{1,0:T(8,128)(2,1)}, u32[]{:S(2)}) copy-start(bf16[1024,1024]{1,0:T(8,128)(2,1)} %param.5) | copy-start | bytes 6291460
Sparse Core Ops, SparseCore 0:
  19.3 83.4 all-gather.3
  107.4 101.9 all-reduce.3
  223.6 16.3 reduce-scatter.2
  288.2 86.1 all-reduce.5
  377.0 7.4 reduce-scatter.4
  387.4 70.9 all-reduce.7
Sparse Core Ops, SparseCore 1:
  226.4 36.4 all-gather.5
where the time goes:
time: 470 us; the launch traced here: 469 us
  waiting for transfers between devices  336 us (71%)
  matrix products  45.3 us (10%)
  local copies, waits for them, and re-layouts  45.2 us (10%)
  other arithmetic  16.9 us (4%)
  between operations  15.7 us (3%)
  blocking collectives  8.77 us (2%)
    psum x2, waiting for transfers between devices, broadcast(): return lax.psum(jnp.where(mine, array, jnp.zeros_like(array)), axis)  153 us
    all_gather x1, waiting for transfers between devices, shards(): left_feats = lax.all_gather(own_part, 'tcol', axis=1, tiled=True)  83.6 us
    psum x1, waiting for transfers between devices, shards(): lax.psum(curv_local.astype(jnp.bfloat16), 'tcol').astype(jnp.float32)  81.5 us
    gather x1, local copies, waits for them, and re-layouts, shards(): jnp.diagonal(diag_block) * (row_idx == col_idx).astype(jnp.float32)  16.8 us
    reduce_scatter x1, waiting for transfers between devices, shards(): lax.psum_scatter((lax.dot_general(left_feats, right_feats, contract, pref...  14.2 us
    dot_general x1, matrix products, shards(): lax.dot_general(left_feats, right_feats, contract, preferred_element_type...  14 us
    gather x5, local copies, waits for them, and re-layouts, shards(): chosen = jnp.take(gram_three, sub_index, axis=1)  12.8 us
    dot_general x1, matrix products, shards(): jnp.einsum('rpk,pkc->rpc', chosen, pieces, preferred_element_type=jnp.flo...  10.8 us
  transfers between devices with their start and end apart: 7, of which 6 were waited for; matrix products, arithmetic and copies ran while one was open for 10% of the time, Pallas kernels for 0%

commit v1 on v0

--- a/solution.py
+++ b/solution.py
@@ -9,9 +9,15 @@
 STEP_RATE = 0.5
 
 
+def fit_plane_in(vec, mesh_ax):
+    outcome_arr = lax.all_gather(vec, axis_name=mesh_ax)
+    y2 = jnp.sum(outcome_arr, 0)
+    return y2
+
+
 def broadcast(array, axis, root):
     mine = lax.axis_index(axis) == root
-    return lax.psum(jnp.where(mine, array, jnp.zeros_like(array)), axis)
+    return fit_plane_in(jnp.where(mine, array, jnp.zeros_like(array)), axis)
 
 
 def featurize(embeds, frequencies, phases):

time: 470 us -> 570 us (1.21)
  waiting for transfers between devices: 336 us -> 392 us
  other arithmetic: 16.9 us -> 41.5 us
  local copies, waits for them, and re-layouts: 45.2 us -> 69.1 us
    all_gather x0 -> x2, waiting for transfers between devices: none -> 205 us  [fit_plane_in(): outcome_arr = lax.all_gather(vec, axis_name=mesh_ax)]
    psum x2 -> x0, waiting for transfers between devices: 153 us -> none  [broadcast(): return lax.psum(jnp.where(mine, array, jnp.zeros_like(array)), axis)]
    reduce_sum x0 -> x3, other arithmetic: none -> 24.9 us  [fit_plane_in(): y2 = jnp.sum(outcome_arr, 0)]
    all_gather x0 -> x2, local copies, waits for them, and re-layouts: none -> 17.7 us  [fit_plane_in(): outcome_arr = lax.all_gather(vec, axis_name=mesh_ax)]
    psum x1 -> x0, blocking collectives: 8.77 us -> none  [broadcast(): return lax.psum(jnp.where(mine, array, jnp.zeros_like(array)), axis)]
    transpose x0 -> x1, local copies, waits for them, and re-layouts: none -> 6.82 us  [shards(): jnp.einsum('rpk,pkc->rpc', chosen, pieces, preferred_element_type=jnp.flo...]
    all_gather x0 -> x1, blocking collectives: none -> 6.79 us  [fit_plane_in(): outcome_arr = lax.all_gather(vec, axis_name=mesh_ax)]
  transfers between devices with their start and end apart: 7 -> 7, of which waited for: 6 -> 6; matrix products, arithmetic and copies ran while one was open for 10% -> 14% of each run, Pallas kernels for 0% -> 0%
where the time goes in v1:
time: 570 us; the launch traced here: 568 us
  waiting for transfers between devices  392 us (69%)
  local copies, waits for them, and re-layouts  69.1 us (12%)
  matrix products  42.2 us (7%)
  other arithmetic  41.5 us (7%)
  between operations  15.7 us (3%)
  blocking collectives  6.79 us (1%)
    all_gather x2, waiting for transfers between devices, fit_plane_in(): outcome_arr = lax.all_gather(vec, axis_name=mesh_ax)  205 us
    psum x1, waiting for transfers between devices, shards(): lax.psum(curv_local.astype(jnp.bfloat16), 'tcol').astype(jnp.float32)  84.9 us
    all_gather x1, waiting for transfers between devices, shards(): left_feats = lax.all_gather(own_part, 'tcol', axis=1, tiled=True)  83.6 us
    reduce_sum x3, other arithmetic, fit_plane_in(): y2 = jnp.sum(outcome_arr, 0)  24.9 us
    all_gather x2, local copies, waits for them, and re-layouts, fit_plane_in(): outcome_arr = lax.all_gather(vec, axis_name=mesh_ax)  17.7 us
    gather x1, local copies, waits for them, and re-layouts, shards(): jnp.diagonal(diag_block) * (row_idx == col_idx).astype(jnp.float32)  17.3 us
    reduce_scatter x1, waiting for transfers between devices, shards(): lax.psum_scatter((lax.dot_general(left_feats, right_feats, contract, pref...  14.2 us
    dot_general x1, matrix products, shards(): lax.dot_general(left_feats, right_feats, contract, preferred_element_type...  14 us
  transfers between devices with their start and end apart: 7, of which 6 were waited for; matrix products, arithmetic and copies ran while one was open for 14% of the time, Pallas kernels for 0%

profile of v1, /device:TPU:0, one launch (start us, length us, event | category | flops | bytes accessed | tf_op | source)
XLA Modules:
  0.0 568.0 jit_solution(1629967506376602687)
XLA Ops:
  8.1 1.5 copy-done
  9.6 9.6 %multiply_convert_fusion.1 = bf16[1024,512]{1,0:T(8,128)(2,1)} fusion(bf16[1024,1024]{1,0:T(8,128)(2,1)S(1)} %copy-done, bf16[1024,512]{1,0:T(8,128)(2,1)} %param.6, f32[512]{0:T(512)} %param.7), kind=kOutput, calls=%fused_computation.17 | convolution fusion | flops 1075314688 | bytes 4196352 | tf_op jit(solution)/shard_map/dot_general | solution.py:24
  19.3 83.6 %all-gather.9.cloned.1.call-done = bf16[1024,2048]{1,0:T(8,128)(2,1)} async-done(((bf16[1024,512]{1,0:T(8,128)(2,1)}), bf16[1024,2048]{1,0:T(8,128)(2,1)}) %all-gather.9.cloned.1.call-update) | async-done | bytes 4194320 | tf_op jit(solution)/shard_map/all_gather | solution.py:38
  102.8 4.5 broadcast_select_fusion
  107.4 155.8 %all-gather.11.cloned.1.call-done = bf16[4096,2048]{1,0:T(8,128)(2,1)} async-done(((bf16[1024,2048]{1,0:T(8,128)(2,1)}), bf16[4096,2048]{1,0:T(8,128)(2,1)}) %all-gather.11.cloned.1.call-update) | async-done | bytes 16777232 | tf_op jit(solution)/shard_map/all_gather | solution.py:13
  263.1 12.0 %reduce_sum.36 = bf16[1024,2048]{1,0:T(8,128)(2,1)} reduce(bf16[4,1024,2048]{2,1,0:T(8,128)(2,1)} %bitcast.36, bf16[]{:T(256)} %constant.76.clone.1), dimensions={0}, to_apply=%region_0.1 | reduce | flops 6291456 | bytes 20971522 | tf_op jit(solution)/shard_map/reduce_sum | solution.py:14
  275.2 14.0 %multiply_convert_fusion = bf16[2048,2048]{1,0:T(8,128)(2,1)} fusion(bf16[1024,2048]{1,0:T(8,128)(2,1)} %all-gather.9.cloned.1.call-done, bf16[1024,2048]{1,0:T(8,128)(2,1)} %reduce_sum.36), kind=kOutput, calls=%fused_computation.7 | convolution fusion | flops 8598323200 | bytes 16777216 | tf_op jit(solution)/shard_map/dot_general | solution.py:44
  289.3 1.1 copy-done.2
  290.4 0.8 convert_element_type.69
  291.6 14.2 %reduce-scatter.3.cloned.1.call-done = bf16[1024,2048]{1,0:T(8,128)(2,1)} async-done(((bf16[2048,2048]{1,0:T(8,128)(2,1)}), bf16[1024,2048]{1,0:T(8,128)(2,1)}) %reduce-scatter.3.cloned.1.call-update) | async-done | bytes 4194320 | tf_op jit(solution)/shard_map/reduce_scatter | solution.py:42
  305.8 5.8 %fusion.17 = (bf16[1024,2048]{1,0:T(8,128)(2,1)S(1)}, f32[1024,2048]{1,0:T(8,128)}) fusion(s32[2048]{0:T(1024)S(1)} %iota_add_fusion, s32[1024]{0:T(1024)S(1)} %iota_add_fusion.1, bf16[1024,2048]{1,0:T(8,128)(2,1)} %reduce-scatter.3.cloned.1.call-done), kind=kLoop, calls=%fused_computation.47 | loop fusion | flops 10485760 | bytes 16789504 | tf_op jit(solution)/shard_map/convert_element_type | solution.py:65
  312.3 1.6 copy.33
  313.9 4.4 gather_fusion.2
  318.3 6.1 %gather_fusion.1 = bf16[8,512,1024]{2,1,0:T(8,128)(2,1)} fusion(bf16[512,2,1024]{2,0,1:T(8,128)(2,1)} %bitcast.35, s32[1024]{0:T(1024)S(1)} %pad_clamp_fusion), kind=kCustom, calls=%fused_computation.1 | custom fusion | bytes 16777248 | tf_op jit(solution)/shard_map/jit(_take)/gather | solution.py:72
  324.3 4.3 all-gather.13.cloned.1.call-done
  328.7 10.8 %fusion.5 = bf16[1024,8,250]{2,0,1:T(8,128)(2,1)} fusion(bf16[8,1024,250]{2,1,0:T(8,128)(2,1)} %bitcast.41, bf16[512,8,1024]{2,0,1:T(8,128)(2,1)} %bitcast.37, bf16[512,8,1024]{2,0,1:T(8,128)(2,1)} %bitcast.38, pred[8]{0:T(512)(128)(4,1)S(1)} %compare_and_fusion), kind=kOutput, calls=%fused_computation.12 | convolution fusion | flops 4236247040 | bytes 24969224 | tf_op jit(solution)/shard_map/rpk,pkc->rpc/dot_general | solution.py:73
  339.4 6.8 %copy.22 = bf16[1024,8,250]{0,1,2:T(8,128)(2,1)} copy(bf16[1024,8,250]{2,0,1:T(8,128)(2,1)} %fusion.5) | data formatting | bytes 8192000 | tf_op jit(solution)/shard_map/rpk,pkc->rpc/transpose | solution.py:73
  346.2 3.4 convert_bitcast_fusion
  349.6 0.6 copy.23
  350.2 1.9 convert_element_type.72
  352.2 84.9 %all-reduce.2.cloned.1.call-done = bf16[1024,1000]{0,1:T(8,128)(2,1)} async-done(((bf16[1024,1000]{0,1:T(8,128)(2,1)}), bf16[1024,1000]{0,1:T(8,128)(2,1)}) %all-reduce.2.cloned.1.call-update) | async-done | bytes 2048016 | tf_op jit(solution)/shard_map/psum | solution.py:79
  437.1 3.1 broadcast_select_fusion.1
  440.3 4.5 fusion.6
  444.8 1.3 copy.25
  446.1 5.5 constant_dynamic-slice_fusion
  451.7 17.3 %gather_fusion = f32[1024]{0:T(1024)S(1)} fusion(f32[1024,1024]{1,0:T(8,128)} %constant_dynamic-slice_fusion, s32[1024]{0:T(1024)S(1)} %bitcast.33), kind=kCustom, calls=%fused_computation | custom fusion | bytes 16384 | tf_op jit(solution)/shard_map/jit(diagonal)/cond/branch_0_fun/gather | solution.py:78
  468.9 6.8 %all-gather.3 = bf16[4096]{0:T(1024)(128)(2,1)S(1)} all-gather(bf16[1024]{0:T(1024)(128)(2,1)S(1)} %fusion.10), channel_id=5, replica_groups=mesh['trow'=4,'tcol'=4,'dp'=2] {'trow'}, dimensions={0}, use_global_device_ids=true | all-gather | bytes 10240 | tf_op jit(solution)/shard_map/all_gather | solution.py:13
  475.8 49.3 %all-gather.15.cloned.1.call-done = bf16[4096,1000]{0,1:T(8,128)(2,1)} async-done(((bf16[1024,1000]{0,1:T(8,128)(2,1)}), bf16[4096,1000]{0,1:T(8,128)(2,1)}) %all-gather.15.cloned.1.call-update) | async-done | bytes 8192016 | tf_op jit(solution)/shard_map/all_gather | solution.py:13
  525.0 17.7 %reshape.121 = bf16[4,1024,1000]{1,0,2:T(4,128)(2,1)} reshape(bf16[4096,1000]{0,1:T(8,128)(2,1)} %all-gather.15.cloned.1.call-done) | data formatting | bytes 16384000 | tf_op jit(solution)/shard_map/all_gather | solution.py:13
  542.7 12.8 %reduce_sum.37 = bf16[1024,1000]{0,1:T(8,128)(2,1)} reduce(bf16[4,1024,1000]{1,0,2:T(4,128)(2,1)} %reshape.121, bf16[]{:T(256)} %constant.76.clone.1), dimensions={0}, to_apply=%region_3.4 | reduce | flops 3072000 | bytes 10240002 | tf_op jit(solution)/shard_map/reduce_sum | solution.py:14
  555.5 2.5 divide_subtract_fusion
  558.0 2.5 copy.26
  (37 shorter events, 1.5 us)
Async XLA Ops:
  8.0 1.6 copy-start
  8.0 94.8 %all-gather.9.cloned.1.call-start = ((), (), s32[]{:S(2)}) async-start(), calls=%async_computation.2 | async-start | bytes 5242880 | tf_op jit(solution)/shard_map/all_gather | solution.py:38
  19.2 243.9 %all-gather.11.cloned.1.call-start = ((), (), s32[]{:S(2)}) async-start(), calls=%async_computation.6 | async-start | bytes 20971520 | tf_op jit(solution)/shard_map/all_gather | solution.py:13
  107.3 198.4 %reduce-scatter.3.cloned.1.call-start = ((), (), s32[]{:S(2)}) async-start(), calls=%async_computation.3 | async-start | bytes 12582912 | tf_op jit(solution)/shard_map/reduce_scatter | solution.py:42
  289.2 1.2 copy-start.2
  289.2 39.4 %all-gather.13.cloned.1.call-start = ((), (), s32[]{:S(2)}) async-start(), calls=%async_computation.7 | async-start | bytes 4718592 | tf_op jit(solution)/shard_map/all_gather | solution.py:68
  291.3 145.8 %all-reduce.2.cloned.1.call-start = ((), (), s32[]{:S(2)}) async-start(), calls=%async_computation.4 | async-start | bytes 4096000 | tf_op jit(solution)/shard_map/psum | solution.py:79
  352.1 88.2 %copy-start.4 = (s32[1024]{0:T(1024)S(1)}, s32[1024]{0:T(1024)}, u32[]{:S(2)}) copy-start(s32[1024]{0:T(1024)} %param.8) | copy-start | bytes 12292
  352.1 172.9 %all-gather.15.cloned.1.call-start = ((), (), s32[]{:S(2)}) async-start(), calls=%async_computation.8 | async-start | bytes 10240000 | tf_op jit(solution)/shard_map/all_gather | solution.py:13
  440.2 115.3 %reduce-scatter.5.cloned.1.call-start = ((), (), s32[]{:S(2)}) async-start(), calls=%async_computation.5 | async-start | bytes 1572864 | tf_op jit(solution)/shard_map/reduce_scatter | solution.py:62
  542.7 12.8 %copy-start.3 = (f32[1024,250]{0,1:T(8,128)S(1)}, f32[1024,250]{0,1:T(8,128)}, u32[]{:S(2)}) copy-start(f32[1024,250]{0,1:T(8,128)} %copy.25) | copy-start | bytes 3072004
  542.7 17.8 %copy-start.1 = (bf16[1024,1024]{1,0:T(8,128)(2,1)S(1)}, bf16[1024,1024]{1,0:T(8,128)(2,1)}, u32[]{:S(2)}) copy-start(bf16[1024,1024]{1,0:T(8,128)(2,1)} %param.5) | copy-start | bytes 6291460
Sparse Core Ops, SparseCore 0:
  19.3 83.4 all-gather.8
  107.4 155.6 all-gather.10
  289.3 16.3 reduce-scatter.2
  352.3 84.8 all-reduce.1
  440.3 84.6 all-gather.14
  527.1 8.3 reduce-scatter.4
Sparse Core Ops, SparseCore 1:
  292.2 36.4 all-gather.12
